TPU v7x, 32 devices: a whole 2x2x4 slice. The times are simulated.
32 devices in a mesh: dp: 8 (over z, y), sy: 2 (over x), sx: 2 (over core).
Axes of the slice: x: 2, y: 2, z: 4, core: 2. Of those that a mesh axis runs over, the one named last changes fastest.
Arguments:
- features: bfloat16 [8, 56, 56, 256], P('dp', 'sy', 'sx'), may hold values from -8 to 8
- labels: int32 [8], P('dp'), may hold values from 0 to 999
- grid: int32 [2], replicated, may hold values from 0 to 49
- w_reduce: bfloat16 [3, 256, 64], P(None, None, 'dp'), may hold values from -0.375 to 0.375
- w_spatial: bfloat16 [3, 3, 3, 64, 64], P(None, None, None, None, 'dp'), may hold values from -0.25 to 0.25
- w_expand: bfloat16 [3, 64, 256], P(None, None, 'dp'), may hold values from -0.75 to 0.75
- w_class: bfloat16 [256, 1000], P('dp'), may hold values from -1.5 to 1.5
- dir_reduce: bfloat16 [2, 3, 256, 64], P(None, None, None, 'dp'), may hold values from -6 to 6
- dir_spatial: bfloat16 [2, 3, 3, 3, 64, 64], P(None, None, None, None, None, 'dp'), may hold values from -6 to 6
- dir_expand: bfloat16 [2, 3, 64, 256], P(None, None, None, 'dp'), may hold values from -6 to 6
- dir_class: bfloat16 [2, 256, 1000], P(None, 'dp'), may hold values from -6 to 6
- gain_mid: float32 [3, 2, 64], replicated, may hold values from 0.5 to 1.5
- shift_mid: float32 [3, 2, 64], replicated, may hold values from -3 to 3
- gain_out: float32 [3, 256], replicated, may hold values from 0.5 to 1.5
- shift_out: float32 [3, 256], replicated, may hold values from -3 to 3
Outputs:
- section_out: bfloat16 [8, 56, 56, 256], P('dp', 'sy', 'sx')
- image_loss: float32 [8], P('dp')
- mean_loss: float32 [], replicated
All inputs are finite; a program needn't handle non-finite values.
Results may differ from a plain program's by a relative error of at most 0.012.
Values may be sent and summed in bfloat16 or wider, within the bound.
A program may use at most 64 MiB of HBM per device.

v0:
```python
import jax
import jax.numpy as jnp
from jax import lax
from jax.sharding import PartitionSpec as P

BLOCKS = 3
GRID = 50
EPS_NORM = 1e-06
EPS_BN = 1e-05


def extended(cells, sides, width):
    for axis, dim in sides:
        count = lax.axis_size(axis)
        ends = count - 1
        head = lax.slice_in_dim(cells, 0, width, axis=dim)
        tail = lax.slice_in_dim(cells, cells.shape[dim] - width, cells.shape[dim], axis=dim)
        cells = jnp.concatenate(
            [
                lax.ppermute(tail, axis, [(i, (i + 1) % count) for i in range(ends)]),
                cells,
                lax.ppermute(head, axis, [((i + 1) % count, i) for i in range(ends)]),
            ],
            axis=dim,
        )
    return cells


def coefficients(grid):
    values = grid.astype(jnp.float32)
    alpha = (2.0 * values + 1.0 - GRID) / GRID
    return (alpha[0], alpha[1])


def filter_ratio(base, direction):
    base_norm = jnp.sqrt(jnp.sum(jnp.square(base.astype(jnp.float32)), axis=0, keepdims=True))
    dir_norm = jnp.sqrt(
        jnp.sum(jnp.square(direction.astype(jnp.float32)), axis=0, keepdims=True) + EPS_NORM
    )
    return base_norm / dir_norm


def combine_filters(base, dir_a, dir_b, alpha_a, alpha_b):
    ratio_a = filter_ratio(base, dir_a)
    ratio_b = filter_ratio(base, dir_b)
    value = (
        base.astype(jnp.float32)
        + alpha_a * ratio_a * dir_a.astype(jnp.float32)
        + alpha_b * ratio_b * dir_b.astype(jnp.float32)
    )
    return value.astype(jnp.bfloat16)


def perturbed_product(left, base, dir_a, dir_b, alpha_a, alpha_b):
    local = combine_filters(base, dir_a, dir_b, alpha_a, alpha_b)
    return jnp.dot(
        left, lax.all_gather(local, "dp", axis=1, tiled=True), preferred_element_type=jnp.float32
    )


def normalize(y, gain, shift, count):
    mean = lax.psum(jnp.sum(y, axis=0), ("dp", "sy", "sx")) / count
    centred = y - mean
    var = lax.psum(jnp.sum(centred * centred, axis=0), ("dp", "sy", "sx")) / count
    return centred * lax.rsqrt(var + EPS_BN) * gain + shift


def padded_tile(inner):
    return extended(inner, (("sy", 1), ("sx", 2)), 1)


def per_device(
    features,
    labels,
    grid,
    w_reduce,
    w_spatial,
    w_expand,
    w_class,
    dir_reduce,
    dir_spatial,
    dir_expand,
    dir_class,
    gain_mid,
    shift_mid,
    gain_out,
    shift_out,
):
    alpha_a, alpha_b = coefficients(grid)
    images, rows, cols, width = features.shape
    tiles = lax.axis_size("sy") * lax.axis_size("sx")
    count = images * rows * cols * lax.axis_size("dp") * tiles
    inner_width = w_spatial.shape[3]
    current = features
    for block in range(BLOCKS):
        flat = current.reshape(-1, width)
        first = perturbed_product(
            flat, w_reduce[block], dir_reduce[0, block], dir_reduce[1, block], alpha_a, alpha_b
        )
        first = jax.nn.relu(
            normalize(first, gain_mid[block, 0], shift_mid[block, 0], count)
        ).astype(jnp.bfloat16)
        framed = padded_tile(first.reshape(images, rows, cols, inner_width))
        patches = jnp.concatenate(
            [framed[:, i : i + rows, j : j + cols, :] for i in range(3) for j in range(3)], axis=-1
        )
        patches = patches.reshape(-1, 9 * inner_width)
        spatial_base = w_spatial[block].reshape(9 * inner_width, -1)
        spatial_a = dir_spatial[0, block].reshape(9 * inner_width, -1)
        spatial_b = dir_spatial[1, block].reshape(9 * inner_width, -1)
        second = perturbed_product(patches, spatial_base, spatial_a, spatial_b, alpha_a, alpha_b)
        second = jax.nn.relu(
            normalize(second, gain_mid[block, 1], shift_mid[block, 1], count)
        ).astype(jnp.bfloat16)
        third = perturbed_product(
            second, w_expand[block], dir_expand[0, block], dir_expand[1, block], alpha_a, alpha_b
        )
        third = normalize(third, gain_out[block], shift_out[block], count)
        current = (
            jax.nn.relu(flat.astype(jnp.float32) + third)
            .astype(jnp.bfloat16)
            .reshape(images, rows, cols, width)
        )
    pooled_part = jnp.sum(current.astype(jnp.float32), axis=(1, 2))
    pooled = (lax.psum(pooled_part, ("sy", "sx")) / (rows * cols * tiles)).astype(jnp.bfloat16)
    class_a = dir_class[0]
    class_b = dir_class[1]
    norm_base, norm_a, norm_b = lax.psum(
        (
            jnp.sum(jnp.square(w_class.astype(jnp.float32)), axis=0),
            jnp.sum(jnp.square(class_a.astype(jnp.float32)), axis=0),
            jnp.sum(jnp.square(class_b.astype(jnp.float32)), axis=0),
        ),
        "dp",
    )
    ratio_a = jnp.sqrt(norm_base) / jnp.sqrt(norm_a + EPS_NORM)
    ratio_b = jnp.sqrt(norm_base) / jnp.sqrt(norm_b + EPS_NORM)
    local_class = (
        w_class.astype(jnp.float32)
        + alpha_a * ratio_a * class_a.astype(jnp.float32)
        + alpha_b * ratio_b * class_b.astype(jnp.float32)
    ).astype(jnp.bfloat16)
    logits = jnp.dot(
        pooled,
        lax.all_gather(local_class, "dp", axis=0, tiled=True),
        preferred_element_type=jnp.float32,
    )
    summed = jnp.log(jnp.sum(jnp.exp(logits), axis=1))
    classes = lax.broadcasted_iota(jnp.int32, logits.shape, 1)
    picked = jnp.sum(jnp.where(classes == labels[:, None], logits, 0.0), axis=1)
    image_loss = summed - picked
    mean_loss = lax.psum(jnp.sum(image_loss), "dp") / (images * lax.axis_size("dp"))
    return (current, image_loss, mean_loss)


def solution(mesh):
    in_specs = (
        P("dp", "sy", "sx", None),
        P("dp"),
        P(),
        P(None, None, "dp"),
        P(None, None, None, None, "dp"),
        P(None, None, "dp"),
        P("dp", None),
        P(None, None, None, "dp"),
        P(None, None, None, None, None, "dp"),
        P(None, None, None, "dp"),
        P(None, "dp", None),
        P(),
        P(),
        P(),
        P(),
    )
    out_specs = (P("dp", "sy", "sx", None), P("dp"), P())
    return jax.shard_map(
        per_device, mesh=mesh, in_specs=in_specs, out_specs=out_specs, check_vma=False
    )
```

profile of v0, /device:TPU:0, one launch (start us, length us, event | category | flops | bytes accessed | tf_op | source)
XLA Modules:
  0.0 1203.1 jit_solution(10325314932056759414)
XLA Ops:
  42.7 39.6 %psum.161 = f32[64]{0:T(128)S(1)} all-reduce(f32[64]{0:T(128)S(1)} %get-tuple-element.142), channel_id=1, replica_groups=mesh['dp'=8,'sy'=2,'sx'=2] {'dp','sy','sx'}, use_global_device_ids=true, to_apply=%region_4.0 | all-reduce | flops 64 | bytes 512 | tf_op jit(solution)/shard_map/psum | solution.py:62
  82.4 40.7 %psum.162 = f32[64]{0:T(128)S(1)} all-reduce(f32[64]{0:T(128)S(1)} %multiply_reduce_fusion.8), channel_id=1, replica_groups=mesh['dp'=8,'sy'=2,'sx'=2] {'dp','sy','sx'}, use_global_device_ids=true, to_apply=%region_6.0 | all-reduce | flops 64 | bytes 512 | tf_op jit(solution)/shard_map/psum | solution.py:64
  130.6 32.7 %all_gather.31 = bf16[576,64]{0,1:T(8,128)(2,1)} all-gather(bf16[576,8]{0,1:T(8,128)(2,1)S(1)} %add_convert_fusion.2), channel_id=1, replica_groups=mesh['dp'=8,'sy'=2,'sx'=2] {'dp'}, dimensions={1}, use_global_device_ids=true | all-gather | bytes 82944 | tf_op jit(solution)/shard_map/all_gather | solution.py:57
  166.4 32.6 %all_gather.34 = bf16[576,64]{0,1:T(8,128)(2,1)} all-gather(bf16[576,8]{0,1:T(8,128)(2,1)S(1)} %add_convert_fusion.1), channel_id=1, replica_groups=mesh['dp'=8,'sy'=2,'sx'=2] {'dp'}, dimensions={1}, use_global_device_ids=true | all-gather | bytes 82944 | tf_op jit(solution)/shard_map/all_gather | solution.py:57
  200.1 36.1 %all-reduce = (f32[1000]{0:T(1024)S(1)}, f32[1000]{0:T(1024)S(1)}, f32[1000]{0:T(1024)S(1)}) all-reduce(f32[1000]{0:T(1024)S(1)} %get-tuple-element.4, f32[1000]{0:T(1024)S(1)} %get-tuple-element.174, f32[1000]{0:T(1024)S(1)} %get-tuple-element.3), channel_id=1, replica_groups=mesh['dp'=8,'sy'=2,'sx'=2] {'dp'}, use_global_device_ids=true, to_apply=%region_70.71 | all-reduce | flops 3000 | bytes 24000 | tf_op jit(solution)/shard_map/psum | solution.py:128
  348.3 37.4 %psum.163 = f32[64]{0:T(128)S(1)} all-reduce(f32[64]{0:T(128)S(1)} %get-tuple-element.144), channel_id=1, replica_groups=mesh['dp'=8,'sy'=2,'sx'=2] {'dp','sy','sx'}, use_global_device_ids=true, to_apply=%region_11.12 | all-reduce | flops 64 | bytes 512 | tf_op jit(solution)/shard_map/psum | solution.py:62
  386.0 42.8 %psum.164 = f32[64]{0:T(128)S(1)} all-reduce(f32[64]{0:T(128)S(1)} %multiply_reduce_fusion.7), channel_id=1, replica_groups=mesh['dp'=8,'sy'=2,'sx'=2] {'dp','sy','sx'}, use_global_device_ids=true, to_apply=%region_13.14 | all-reduce | flops 64 | bytes 512 | tf_op jit(solution)/shard_map/psum | solution.py:64
  429.9 38.1 %psum.165 = f32[256]{0:T(256)S(1)} all-reduce(f32[256]{0:T(256)S(1)} %get-tuple-element.146), channel_id=1, replica_groups=mesh['dp'=8,'sy'=2,'sx'=2] {'dp','sy','sx'}, use_global_device_ids=true, to_apply=%region_18.19 | all-reduce | flops 256 | bytes 2048 | tf_op jit(solution)/shard_map/psum | solution.py:62
  468.1 41.9 %psum.166 = f32[256]{0:T(256)S(1)} all-reduce(f32[256]{0:T(256)S(1)} %multiply_reduce_fusion.2), channel_id=1, replica_groups=mesh['dp'=8,'sy'=2,'sx'=2] {'dp','sy','sx'}, use_global_device_ids=true, to_apply=%region_20.21 | all-reduce | flops 256 | bytes 2048 | tf_op jit(solution)/shard_map/psum | solution.py:64
  511.8 38.3 %psum.167 = f32[64]{0:T(128)S(1)} all-reduce(f32[64]{0:T(128)S(1)} %get-tuple-element.148), channel_id=1, replica_groups=mesh['dp'=8,'sy'=2,'sx'=2] {'dp','sy','sx'}, use_global_device_ids=true, to_apply=%region_25.26 | all-reduce | flops 64 | bytes 512 | tf_op jit(solution)/shard_map/psum | solution.py:62
  550.2 41.9 %psum.168 = f32[64]{0:T(128)S(1)} all-reduce(f32[64]{0:T(128)S(1)} %multiply_reduce_fusion.6), channel_id=1, replica_groups=mesh['dp'=8,'sy'=2,'sx'=2] {'dp','sy','sx'}, use_global_device_ids=true, to_apply=%region_27.28 | all-reduce | flops 64 | bytes 512 | tf_op jit(solution)/shard_map/psum | solution.py:64
  597.3 32.5 %all_gather.35 = bf16[64,256]{0,1:T(8,128)(2,1)} all-gather(bf16[64,32]{0,1:T(8,128)(2,1)S(1)} %copy-done.24), channel_id=1, replica_groups=mesh['dp'=8,'sy'=2,'sx'=2] {'dp'}, dimensions={1}, use_global_device_ids=true | all-gather | bytes 36864 | tf_op jit(solution)/shard_map/all_gather | solution.py:57
  679.1 36.9 %psum.169 = f32[64]{0:T(128)S(1)} all-reduce(f32[64]{0:T(128)S(1)} %get-tuple-element.150), channel_id=1, replica_groups=mesh['dp'=8,'sy'=2,'sx'=2] {'dp','sy','sx'}, use_global_device_ids=true, to_apply=%region_32.33 | all-reduce | flops 64 | bytes 512 | tf_op jit(solution)/shard_map/psum | solution.py:62
  716.2 41.0 %psum.170 = f32[64]{0:T(128)S(1)} all-reduce(f32[64]{0:T(128)S(1)} %multiply_reduce_fusion.5), channel_id=1, replica_groups=mesh['dp'=8,'sy'=2,'sx'=2] {'dp','sy','sx'}, use_global_device_ids=true, to_apply=%region_34.35 | all-reduce | flops 64 | bytes 512 | tf_op jit(solution)/shard_map/psum | solution.py:64
  758.3 39.7 %psum.171 = f32[256]{0:T(256)S(1)} all-reduce(f32[256]{0:T(256)S(1)} %get-tuple-element.152), channel_id=1, replica_groups=mesh['dp'=8,'sy'=2,'sx'=2] {'dp','sy','sx'}, use_global_device_ids=true, to_apply=%region_39.40 | all-reduce | flops 256 | bytes 2048 | tf_op jit(solution)/shard_map/psum | solution.py:62
  798.1 40.3 %psum.172 = f32[256]{0:T(256)S(1)} all-reduce(f32[256]{0:T(256)S(1)} %multiply_reduce_fusion.1), channel_id=1, replica_groups=mesh['dp'=8,'sy'=2,'sx'=2] {'dp','sy','sx'}, use_global_device_ids=true, to_apply=%region_41.42 | all-reduce | flops 256 | bytes 2048 | tf_op jit(solution)/shard_map/psum | solution.py:64
  839.7 39.7 %psum.173 = f32[64]{0:T(128)S(1)} all-reduce(f32[64]{0:T(128)S(1)} %get-tuple-element.154), channel_id=1, replica_groups=mesh['dp'=8,'sy'=2,'sx'=2] {'dp','sy','sx'}, use_global_device_ids=true, to_apply=%region_46.47 | all-reduce | flops 64 | bytes 512 | tf_op jit(solution)/shard_map/psum | solution.py:62
  879.5 40.3 %psum.174 = f32[64]{0:T(128)S(1)} all-reduce(f32[64]{0:T(128)S(1)} %multiply_reduce_fusion.4), channel_id=1, replica_groups=mesh['dp'=8,'sy'=2,'sx'=2] {'dp','sy','sx'}, use_global_device_ids=true, to_apply=%region_48.49 | all-reduce | flops 64 | bytes 512 | tf_op jit(solution)/shard_map/psum | solution.py:64
  925.1 32.5 %all_gather.37 = bf16[576,64]{0,1:T(8,128)(2,1)} all-gather(bf16[576,8]{0,1:T(8,128)(2,1)S(1)} %add_convert_fusion), channel_id=1, replica_groups=mesh['dp'=8,'sy'=2,'sx'=2] {'dp'}, dimensions={1}, use_global_device_ids=true | all-gather | bytes 82944 | tf_op jit(solution)/shard_map/all_gather | solution.py:57
  966.0 32.8 %all_gather.38 = bf16[64,256]{0,1:T(8,128)(2,1)} all-gather(bf16[64,32]{0,1:T(8,128)(2,1)S(1)} %copy-done.23), channel_id=1, replica_groups=mesh['dp'=8,'sy'=2,'sx'=2] {'dp'}, dimensions={1}, use_global_device_ids=true | all-gather | bytes 36864 | tf_op jit(solution)/shard_map/all_gather | solution.py:57
  1008.1 36.9 %psum.175 = f32[64]{0:T(128)S(1)} all-reduce(f32[64]{0:T(128)S(1)} %get-tuple-element.156), channel_id=1, replica_groups=mesh['dp'=8,'sy'=2,'sx'=2] {'dp','sy','sx'}, use_global_device_ids=true, to_apply=%region_53.54 | all-reduce | flops 64 | bytes 512 | tf_op jit(solution)/shard_map/psum | solution.py:62
  1045.2 41.8 %psum.176 = f32[64]{0:T(128)S(1)} all-reduce(f32[64]{0:T(128)S(1)} %multiply_reduce_fusion.3), channel_id=1, replica_groups=mesh['dp'=8,'sy'=2,'sx'=2] {'dp','sy','sx'}, use_global_device_ids=true, to_apply=%region_55.56 | all-reduce | flops 64 | bytes 512 | tf_op jit(solution)/shard_map/psum | solution.py:64
  1088.1 38.9 %psum.177 = f32[256]{0:T(256)S(1)} all-reduce(f32[256]{0:T(256)S(1)} %get-tuple-element.158), channel_id=1, replica_groups=mesh['dp'=8,'sy'=2,'sx'=2] {'dp','sy','sx'}, use_global_device_ids=true, to_apply=%region_60.61 | all-reduce | flops 256 | bytes 2048 | tf_op jit(solution)/shard_map/psum | solution.py:62
  1127.2 41.2 %psum.178 = f32[256]{0:T(256)S(1)} all-reduce(f32[256]{0:T(256)S(1)} %multiply_reduce_fusion), channel_id=1, replica_groups=mesh['dp'=8,'sy'=2,'sx'=2] {'dp','sy','sx'}, use_global_device_ids=true, to_apply=%region_62.63 | all-reduce | flops 256 | bytes 2048 | tf_op jit(solution)/shard_map/psum | solution.py:64
  (334 shorter events, 280.2 us)
Async XLA Ops:
  82.2 40.9 %copy-start.42 = (f32[3,2,64]{2,1,0:T(2,128)S(1)}, f32[3,2,64]{2,1,0:T(2,128)}, u32[]{:S(2)}) copy-start(f32[3,2,64]{2,1,0:T(2,128)} %param.26) | copy-start | bytes 4612
  82.4 40.7 %copy-start.41 = (f32[3,2,64]{2,1,0:T(2,128)S(1)}, f32[3,2,64]{2,1,0:T(2,128)}, u32[]{:S(2)}) copy-start(f32[3,2,64]{2,1,0:T(2,128)} %param.27) | copy-start | bytes 4612
  124.6 5.6 copy-start.9
  124.7 180.1 %collective-permute-start = (bf16[1,1,28,64]{3,2,1,0:T(8,128)(2,1)S(1)}, bf16[1,1,28,64]{3,2,1,0:T(8,128)(2,1)S(1)}, u32[]{:S(2)}, u32[]{:S(2)}) collective-permute-start(bf16[1,1,28,64]{3,2,1,0:T(8,128)(2,1)S(1)} %get-tuple-element.86), channel_id=1, source_target_pairs={{0,2},{1,3},{4,6},{5,7},{8,10},{9,11},{12,14},{13,15},{16,18},{17,... | collective-permute-start | bytes 10760 | tf_op jit(solution)/shard_map/ppermute | solution.py:20
  128.8 175.9 %collective-permute-start.1 = (bf16[1,1,28,64]{3,2,1,0:T(8,128)(2,1)S(1)}, bf16[1,1,28,64]{3,2,1,0:T(8,128)(2,1)S(1)}, u32[]{:S(2)}, u32[]{:S(2)}) collective-permute-start(bf16[1,1,28,64]{3,2,1,0:T(8,128)(2,1)S(1)} %get-tuple-element.85), channel_id=1, source_target_pairs={{2,0},{3,1},{6,4},{7,5},{10,8},{11,9},{14,12},{15,13},{18,16},{19,... | collective-permute-start | bytes 10760 | tf_op jit(solution)/shard_map/ppermute | solution.py:22
  130.6 32.7 %copy-start.18 = (bf16[2,3,64,32]{2,3,1,0:T(8,128)(2,1)S(1)}, bf16[2,3,64,32]{2,3,1,0:T(8,128)(2,1)}, u32[]{:S(2)}) copy-start(bf16[2,3,64,32]{2,3,1,0:T(8,128)(2,1)} %param.24) | copy-start | bytes 73732
  304.9 36.4 %collective-permute-start.2 = (bf16[1,30,1,64]{3,2,1,0:T(2,128)(2,1)S(1)}, bf16[1,30,1,64]{3,2,1,0:T(2,128)(2,1)S(1)}, u32[]{:S(2)}, u32[]{:S(2)}) collective-permute-start(bf16[1,30,1,64]{3,2,1,0:T(2,128)(2,1)S(1)} %get-tuple-element.71), channel_id=1, source_target_pairs={{0,1},{2,3},{4,5},{6,7},{8,9},{10,11},{12,13},{14,15},{16,17},{18,... | collective-permute-start | bytes 11528 | tf_op jit(solution)/shard_map/ppermute | solution.py:20
  306.2 35.1 %collective-permute-start.3 = (bf16[1,30,1,64]{3,2,1,0:T(2,128)(2,1)S(1)}, bf16[1,30,1,64]{3,2,1,0:T(2,128)(2,1)S(1)}, u32[]{:S(2)}, u32[]{:S(2)}) collective-permute-start(bf16[1,30,1,64]{3,2,1,0:T(2,128)(2,1)S(1)} %get-tuple-element.70), channel_id=1, source_target_pairs={{1,0},{3,2},{5,4},{7,6},{9,8},{11,10},{13,12},{15,14},{17,16},{19,... | collective-permute-start | bytes 11528 | tf_op jit(solution)/shard_map/ppermute | solution.py:22
  385.8 43.0 %copy-start.14 = (bf16[64,256]{0,1:T(8,128)(2,1)S(1)}, bf16[64,256]{0,1:T(8,128)(2,1)}, u32[]{:S(2)}) copy-start(bf16[64,256]{0,1:T(8,128)(2,1)} %all_gather.32) | copy-start | bytes 98308
  468.0 42.0 %copy-start.38 = (f32[1,256]{1,0:T(1,128)S(1)}, f32[1,256]{1,0:T(1,128)}, u32[]{:S(2)}) copy-start(f32[1,256]{1,0:T(1,128)} %get-tuple-element.108) | copy-start | bytes 3076
  593.0 4.3 copy-start.24
  593.1 38.0 %collective-permute-start.4 = (bf16[1,1,28,64]{3,2,1,0:T(8,128)(2,1)S(1)}, bf16[1,1,28,64]{3,2,1,0:T(8,128)(2,1)S(1)}, u32[]{:S(2)}, u32[]{:S(2)}) collective-permute-start(bf16[1,1,28,64]{3,2,1,0:T(8,128)(2,1)S(1)} %get-tuple-element.81), channel_id=1, source_target_pairs={{0,2},{1,3},{4,6},{5,7},{8,10},{9,11},{12,14},{13,15},{16,18},{17,... | collective-permute-start | bytes 10760 | tf_op jit(solution)/shard_map/ppermute | solution.py:20
  629.9 5.5 collective-permute-start.5
  635.6 34.3 %collective-permute-start.6 = (bf16[1,30,1,64]{3,2,1,0:T(2,128)(2,1)S(1)}, bf16[1,30,1,64]{3,2,1,0:T(2,128)(2,1)S(1)}, u32[]{:S(2)}, u32[]{:S(2)}) collective-permute-start(bf16[1,30,1,64]{3,2,1,0:T(2,128)(2,1)S(1)} %get-tuple-element.66), channel_id=1, source_target_pairs={{0,1},{2,3},{4,5},{6,7},{8,9},{10,11},{12,13},{14,15},{16,17},{18,... | collective-permute-start | bytes 11528 | tf_op jit(solution)/shard_map/ppermute | solution.py:20
  636.9 33.0 %collective-permute-start.7 = (bf16[1,30,1,64]{3,2,1,0:T(2,128)(2,1)S(1)}, bf16[1,30,1,64]{3,2,1,0:T(2,128)(2,1)S(1)}, u32[]{:S(2)}, u32[]{:S(2)}) collective-permute-start(bf16[1,30,1,64]{3,2,1,0:T(2,128)(2,1)S(1)} %get-tuple-element.65), channel_id=1, source_target_pairs={{1,0},{3,2},{5,4},{7,6},{9,8},{11,10},{13,12},{15,14},{17,16},{19,... | collective-permute-start | bytes 11528 | tf_op jit(solution)/shard_map/ppermute | solution.py:22
  716.0 41.2 %copy-start.13 = (bf16[64,256]{0,1:T(8,128)(2,1)S(1)}, bf16[64,256]{0,1:T(8,128)(2,1)}, u32[]{:S(2)}) copy-start(bf16[64,256]{0,1:T(8,128)(2,1)} %all_gather.35) | copy-start | bytes 98308
  798.0 40.4 %copy-start.36 = (f32[1,256]{1,0:T(1,128)S(1)}, f32[1,256]{1,0:T(1,128)}, u32[]{:S(2)}) copy-start(f32[1,256]{1,0:T(1,128)} %get-tuple-element.107) | copy-start | bytes 3076
  920.9 38.0 %collective-permute-start.8 = (bf16[1,1,28,64]{3,2,1,0:T(8,128)(2,1)S(1)}, bf16[1,1,28,64]{3,2,1,0:T(8,128)(2,1)S(1)}, u32[]{:S(2)}, u32[]{:S(2)}) collective-permute-start(bf16[1,1,28,64]{3,2,1,0:T(8,128)(2,1)S(1)} %get-tuple-element.76), channel_id=1, source_target_pairs={{0,2},{1,3},{4,6},{5,7},{8,10},{9,11},{12,14},{13,15},{16,18},{17,... | collective-permute-start | bytes 10760 | tf_op jit(solution)/shard_map/ppermute | solution.py:20
  957.6 5.5 collective-permute-start.9
  963.3 2.6 copy-start.23
  963.4 37.7 %collective-permute-start.10 = (bf16[1,30,1,64]{3,2,1,0:T(2,128)(2,1)S(1)}, bf16[1,30,1,64]{3,2,1,0:T(2,128)(2,1)S(1)}, u32[]{:S(2)}, u32[]{:S(2)}) collective-permute-start(bf16[1,30,1,64]{3,2,1,0:T(2,128)(2,1)S(1)} %get-tuple-element.61), channel_id=1, source_target_pairs={{0,1},{2,3},{4,5},{6,7},{8,9},{10,11},{12,13},{14,15},{16,17},{18,... | collective-permute-start | bytes 11528 | tf_op jit(solution)/shard_map/ppermute | solution.py:20
  964.7 36.4 %collective-permute-start.11 = (bf16[1,30,1,64]{3,2,1,0:T(2,128)(2,1)S(1)}, bf16[1,30,1,64]{3,2,1,0:T(2,128)(2,1)S(1)}, u32[]{:S(2)}, u32[]{:S(2)}) collective-permute-start(bf16[1,30,1,64]{3,2,1,0:T(2,128)(2,1)S(1)} %get-tuple-element.60), channel_id=1, source_target_pairs={{1,0},{3,2},{5,4},{7,6},{9,8},{11,10},{13,12},{15,14},{17,16},{19,... | collective-permute-start | bytes 11528 | tf_op jit(solution)/shard_map/ppermute | solution.py:22
  1045.0 42.0 %copy-start.15 = (bf16[64,256]{0,1:T(8,128)(2,1)S(1)}, bf16[64,256]{0,1:T(8,128)(2,1)}, u32[]{:S(2)}) copy-start(bf16[64,256]{0,1:T(8,128)(2,1)} %all_gather.38) | copy-start | bytes 98308
  1127.0 41.3 %copy-start.40 = (f32[1,256]{1,0:T(1,128)S(1)}, f32[1,256]{1,0:T(1,128)}, u32[]{:S(2)}) copy-start(f32[1,256]{1,0:T(1,128)} %get-tuple-element.109) | copy-start | bytes 3076
  (45 other events, 34.6 us)
where the time goes:
time: 1210 us; the launch traced here: 1200 us
  blocking collectives  1100 us (91%)
  local copies, waits for them, and re-layouts  39.7 us (3%)
  starting transfers between devices  24.1 us (2%)
  other arithmetic  17.3 us (1%)
    psum x9, blocking collectives, normalize(): lax.psum(jnp.sum(centred * centred, axis=0), ('dp', 'sy', 'sx')) / count  372 us
    psum x9, blocking collectives, normalize(): mean = lax.psum(jnp.sum(y, axis=0), ('dp', 'sy', 'sx')) / count  345 us
    all_gather x9, blocking collectives, perturbed_product(): lax.all_gather(local, 'dp', axis=1, tiled=True)  291 us
    psum x1, blocking collectives, per_device(): lax.psum((jnp.sum(jnp.square(w_class.astype(jnp.float32)), axis=0), jnp.s...  36.1 us
    all_gather x1, blocking collectives, per_device(): lax.all_gather(local_class, 'dp', axis=0, tiled=True)  31.2 us
  transfers between devices with their start and end apart: 12, of which 2 were waited for; matrix products, arithmetic and copies ran while one was open for 1% of the time, Pallas kernels for 0%

commit v1 on v0

--- a/solution.py
+++ b/solution.py
@@ -61,7 +61,10 @@
 def normalize(y, gain, shift, count):
     mean = lax.psum(jnp.sum(y, axis=0), ("dp", "sy", "sx")) / count
     centred = y - mean
-    var = lax.psum(jnp.sum(centred * centred, axis=0), ("dp", "sy", "sx")) / count
+    var = (
+        jnp.sum(lax.all_gather(jnp.sum(centred * centred, axis=0), ("dp", "sy", "sx")), axis=0)
+        / count
+    )
     return centred * lax.rsqrt(var + EPS_BN) * gain + shift
 
 

time: 1210 us -> 1200 us (level)
    psum x9 -> x0, blocking collectives: 372 us -> none  [normalize(): lax.psum(jnp.sum(centred * centred, axis=0), ('dp', 'sy', 'sx')) / count]
    unnamed x0 -> x6, blocking collectives: none -> 249 us
    all_gather x0 -> x3, blocking collectives: none -> 122 us  [normalize(): lax.all_gather(jnp.sum(centred * centred, axis=0), ('dp', 'sy', 'sx'))]
where the time goes in v1:
time: 1200 us
  blocking collectives  1090 us (91%)
  local copies, waits for them, and re-layouts  42.9 us (4%)
  starting transfers between devices  24.1 us (2%)
  other arithmetic  17 us (1%)
    psum x9, blocking collectives, normalize(): mean = lax.psum(jnp.sum(y, axis=0), ('dp', 'sy', 'sx')) / count  341 us
    all_gather x9, blocking collectives, perturbed_product(): lax.all_gather(local, 'dp', axis=1, tiled=True)  291 us
    unnamed x6, blocking collectives  249 us
    all_gather x3, blocking collectives, normalize(): lax.all_gather(jnp.sum(centred * centred, axis=0), ('dp', 'sy', 'sx'))  122 us
    psum x1, blocking collectives, per_device(): lax.psum((jnp.sum(jnp.square(w_class.astype(jnp.float32)), axis=0), jnp.s...  36.1 us
    all_gather x1, blocking collectives, per_device(): lax.all_gather(local_class, 'dp', axis=0, tiled=True)  31.2 us
    unnamed x152, local copies, waits for them, and re-layouts  24 us
  transfers between devices with their start and end apart: 12, of which 2 were waited for; matrix products, arithmetic and copies ran while one was open for 1% of the time, Pallas kernels for 0%

profile of v1, /device:TPU:0, one launch (start us, length us, event | category | flops | bytes accessed | tf_op | source)
XLA Modules:
  0.0 1197.8 jit_solution(7910299120495825022)
XLA Ops:
  42.7 39.5 %psum.98 = f32[64]{0:T(128)S(1)} all-reduce(f32[64]{0:T(128)S(1)} %get-tuple-element.142), channel_id=1, replica_groups=mesh['dp'=8,'sy'=2,'sx'=2] {'dp','sy','sx'}, use_global_device_ids=true, to_apply=%region_4.0 | all-reduce | flops 64 | bytes 512 | tf_op jit(solution)/shard_map/psum | solution.py:62
  82.7 40.6 %all-reduce = f32[2048]{0:T(1024)S(1)} all-reduce(f32[2048]{0:T(1024)S(1)} %dynamic-update-slice), channel_id=2, replica_groups=mesh['dp'=8,'sy'=2,'sx'=2] {'dp','sy','sx'}, use_global_device_ids=true, to_apply=%add | all-reduce | flops 2048 | bytes 16384
  131.5 32.7 %all_gather.87 = bf16[576,64]{0,1:T(8,128)(2,1)} all-gather(bf16[576,8]{0,1:T(8,128)(2,1)S(1)} %add_convert_fusion.2), channel_id=1, replica_groups=mesh['dp'=8,'sy'=2,'sx'=2] {'dp'}, dimensions={1}, use_global_device_ids=true | all-gather | bytes 82944 | tf_op jit(solution)/shard_map/all_gather | solution.py:57
  167.3 32.6 %all_gather.96 = bf16[576,64]{0,1:T(8,128)(2,1)} all-gather(bf16[576,8]{0,1:T(8,128)(2,1)S(1)} %add_convert_fusion.1), channel_id=1, replica_groups=mesh['dp'=8,'sy'=2,'sx'=2] {'dp'}, dimensions={1}, use_global_device_ids=true | all-gather | bytes 82944 | tf_op jit(solution)/shard_map/all_gather | solution.py:57
  201.0 36.1 %all-reduce.6 = (f32[1000]{0:T(1024)S(1)}, f32[1000]{0:T(1024)S(1)}, f32[1000]{0:T(1024)S(1)}) all-reduce(f32[1000]{0:T(1024)S(1)} %get-tuple-element.4, f32[1000]{0:T(1024)S(1)} %get-tuple-element.174, f32[1000]{0:T(1024)S(1)} %get-tuple-element.3), channel_id=1, replica_groups=mesh['dp'=8,'sy'=2,'sx'=2] {'dp'}, use_global_device_ids=true, to_apply=%region_70.71 | all-reduce | flops 3000 | bytes 24000 | tf_op jit(solution)/shard_map/psum | solution.py:131
  349.3 37.4 %psum.99 = f32[64]{0:T(128)S(1)} all-reduce(f32[64]{0:T(128)S(1)} %get-tuple-element.144), channel_id=1, replica_groups=mesh['dp'=8,'sy'=2,'sx'=2] {'dp','sy','sx'}, use_global_device_ids=true, to_apply=%region_11.12 | all-reduce | flops 64 | bytes 512 | tf_op jit(solution)/shard_map/psum | solution.py:62
  387.2 42.8 %all-reduce.1 = f32[2048]{0:T(1024)S(1)} all-reduce(f32[2048]{0:T(1024)S(1)} %dynamic-update-slice.1), channel_id=3, replica_groups=mesh['dp'=8,'sy'=2,'sx'=2] {'dp','sy','sx'}, use_global_device_ids=true, to_apply=%add.1 | all-reduce | flops 2048 | bytes 16384
  431.2 38.1 %psum.100 = f32[256]{0:T(256)S(1)} all-reduce(f32[256]{0:T(256)S(1)} %get-tuple-element.146), channel_id=1, replica_groups=mesh['dp'=8,'sy'=2,'sx'=2] {'dp','sy','sx'}, use_global_device_ids=true, to_apply=%region_18.19 | all-reduce | flops 256 | bytes 2048 | tf_op jit(solution)/shard_map/psum | solution.py:62
  469.5 40.9 %all-gather.9 = f32[32,1,256]{2,1,0:T(1,128)S(1)} all-gather(f32[1,1,256]{2,1,0:T(1,128)S(1)} %bitcast.162), channel_id=4, replica_groups=mesh['dp'=8,'sy'=2,'sx'=2] {'dp','sy','sx'}, dimensions={0}, use_global_device_ids=true | all-gather | bytes 33792 | tf_op jit(solution)/shard_map/all_gather | solution.py:65
  512.2 37.0 %psum.101 = f32[64]{0:T(128)S(1)} all-reduce(f32[64]{0:T(128)S(1)} %get-tuple-element.148), channel_id=1, replica_groups=mesh['dp'=8,'sy'=2,'sx'=2] {'dp','sy','sx'}, use_global_device_ids=true, to_apply=%region_25.26 | all-reduce | flops 64 | bytes 512 | tf_op jit(solution)/shard_map/psum | solution.py:62
  549.7 41.2 %all-reduce.2 = f32[2048]{0:T(1024)S(1)} all-reduce(f32[2048]{0:T(1024)S(1)} %dynamic-update-slice.2), channel_id=5, replica_groups=mesh['dp'=8,'sy'=2,'sx'=2] {'dp','sy','sx'}, use_global_device_ids=true, to_apply=%add.2 | all-reduce | flops 2048 | bytes 16384
  596.3 32.5 %all_gather.99 = bf16[64,256]{0,1:T(8,128)(2,1)} all-gather(bf16[64,32]{0,1:T(8,128)(2,1)S(1)} %copy-done.24), channel_id=1, replica_groups=mesh['dp'=8,'sy'=2,'sx'=2] {'dp'}, dimensions={1}, use_global_device_ids=true | all-gather | bytes 36864 | tf_op jit(solution)/shard_map/all_gather | solution.py:57
  678.1 36.9 %psum.102 = f32[64]{0:T(128)S(1)} all-reduce(f32[64]{0:T(128)S(1)} %get-tuple-element.150), channel_id=1, replica_groups=mesh['dp'=8,'sy'=2,'sx'=2] {'dp','sy','sx'}, use_global_device_ids=true, to_apply=%region_32.33 | all-reduce | flops 64 | bytes 512 | tf_op jit(solution)/shard_map/psum | solution.py:62
  715.5 41.7 %all-reduce.3 = f32[2048]{0:T(1024)S(1)} all-reduce(f32[2048]{0:T(1024)S(1)} %dynamic-update-slice.3), channel_id=6, replica_groups=mesh['dp'=8,'sy'=2,'sx'=2] {'dp','sy','sx'}, use_global_device_ids=true, to_apply=%add.3 | all-reduce | flops 2048 | bytes 16384
  758.4 38.9 %psum.103 = f32[256]{0:T(256)S(1)} all-reduce(f32[256]{0:T(256)S(1)} %get-tuple-element.152), channel_id=1, replica_groups=mesh['dp'=8,'sy'=2,'sx'=2] {'dp','sy','sx'}, use_global_device_ids=true, to_apply=%region_39.40 | all-reduce | flops 256 | bytes 2048 | tf_op jit(solution)/shard_map/psum | solution.py:62
  797.5 40.7 %all-gather.10 = f32[32,1,256]{2,1,0:T(1,128)S(1)} all-gather(f32[1,1,256]{2,1,0:T(1,128)S(1)} %bitcast.163), channel_id=7, replica_groups=mesh['dp'=8,'sy'=2,'sx'=2] {'dp','sy','sx'}, dimensions={0}, use_global_device_ids=true | all-gather | bytes 33792 | tf_op jit(solution)/shard_map/all_gather | solution.py:65
  839.5 36.8 %psum.104 = f32[64]{0:T(128)S(1)} all-reduce(f32[64]{0:T(128)S(1)} %get-tuple-element.154), channel_id=1, replica_groups=mesh['dp'=8,'sy'=2,'sx'=2] {'dp','sy','sx'}, use_global_device_ids=true, to_apply=%region_46.47 | all-reduce | flops 64 | bytes 512 | tf_op jit(solution)/shard_map/psum | solution.py:62
  876.8 41.2 %all-reduce.4 = f32[2048]{0:T(1024)S(1)} all-reduce(f32[2048]{0:T(1024)S(1)} %dynamic-update-slice.4), channel_id=8, replica_groups=mesh['dp'=8,'sy'=2,'sx'=2] {'dp','sy','sx'}, use_global_device_ids=true, to_apply=%add.4 | all-reduce | flops 2048 | bytes 16384
  923.4 32.5 %all_gather.105 = bf16[576,64]{0,1:T(8,128)(2,1)} all-gather(bf16[576,8]{0,1:T(8,128)(2,1)S(1)} %add_convert_fusion), channel_id=1, replica_groups=mesh['dp'=8,'sy'=2,'sx'=2] {'dp'}, dimensions={1}, use_global_device_ids=true | all-gather | bytes 82944 | tf_op jit(solution)/shard_map/all_gather | solution.py:57
  964.2 32.8 %all_gather.108 = bf16[64,256]{0,1:T(8,128)(2,1)} all-gather(bf16[64,32]{0,1:T(8,128)(2,1)S(1)} %copy-done.23), channel_id=1, replica_groups=mesh['dp'=8,'sy'=2,'sx'=2] {'dp'}, dimensions={1}, use_global_device_ids=true | all-gather | bytes 36864 | tf_op jit(solution)/shard_map/all_gather | solution.py:57
  1006.4 37.0 %psum.105 = f32[64]{0:T(128)S(1)} all-reduce(f32[64]{0:T(128)S(1)} %get-tuple-element.156), channel_id=1, replica_groups=mesh['dp'=8,'sy'=2,'sx'=2] {'dp','sy','sx'}, use_global_device_ids=true, to_apply=%region_53.54 | all-reduce | flops 64 | bytes 512 | tf_op jit(solution)/shard_map/psum | solution.py:62
  1043.8 41.7 %all-reduce.5 = f32[2048]{0:T(1024)S(1)} all-reduce(f32[2048]{0:T(1024)S(1)} %dynamic-update-slice.5), channel_id=9, replica_groups=mesh['dp'=8,'sy'=2,'sx'=2] {'dp','sy','sx'}, use_global_device_ids=true, to_apply=%add.5 | all-reduce | flops 2048 | bytes 16384
  1086.7 39.0 %psum.106 = f32[256]{0:T(256)S(1)} all-reduce(f32[256]{0:T(256)S(1)} %get-tuple-element.158), channel_id=1, replica_groups=mesh['dp'=8,'sy'=2,'sx'=2] {'dp','sy','sx'}, use_global_device_ids=true, to_apply=%region_60.61 | all-reduce | flops 256 | bytes 2048 | tf_op jit(solution)/shard_map/psum | solution.py:62
  1125.8 40.7 %all-gather.11 = f32[32,1,256]{2,1,0:T(1,128)S(1)} all-gather(f32[1,1,256]{2,1,0:T(1,128)S(1)} %bitcast.164), channel_id=10, replica_groups=mesh['dp'=8,'sy'=2,'sx'=2] {'dp','sy','sx'}, dimensions={0}, use_global_device_ids=true | all-gather | bytes 33792 | tf_op jit(solution)/shard_map/all_gather | solution.py:65
  (363 shorter events, 279.5 us)
Async XLA Ops:
  2.8 1.0 copy-start.17
  6.1 2.6 copy-start.20
  125.5 5.6 copy-start.9
  125.6 180.1 %collective-permute-start = (bf16[1,1,28,64]{3,2,1,0:T(8,128)(2,1)S(1)}, bf16[1,1,28,64]{3,2,1,0:T(8,128)(2,1)S(1)}, u32[]{:S(2)}, u32[]{:S(2)}) collective-permute-start(bf16[1,1,28,64]{3,2,1,0:T(8,128)(2,1)S(1)} %get-tuple-element.86), channel_id=1, source_target_pairs={{0,2},{1,3},{4,6},{5,7},{8,10},{9,11},{12,14},{13,15},{16,18},{17,... | collective-permute-start | bytes 10760 | tf_op jit(solution)/shard_map/ppermute | solution.py:20
  129.8 175.9 %collective-permute-start.1 = (bf16[1,1,28,64]{3,2,1,0:T(8,128)(2,1)S(1)}, bf16[1,1,28,64]{3,2,1,0:T(8,128)(2,1)S(1)}, u32[]{:S(2)}, u32[]{:S(2)}) collective-permute-start(bf16[1,1,28,64]{3,2,1,0:T(8,128)(2,1)S(1)} %get-tuple-element.85), channel_id=1, source_target_pairs={{2,0},{3,1},{6,4},{7,5},{10,8},{11,9},{14,12},{15,13},{18,16},{19,... | collective-permute-start | bytes 10760 | tf_op jit(solution)/shard_map/ppermute | solution.py:22
  131.5 32.7 %copy-start.18 = (bf16[2,3,64,32]{2,3,1,0:T(8,128)(2,1)S(1)}, bf16[2,3,64,32]{2,3,1,0:T(8,128)(2,1)}, u32[]{:S(2)}) copy-start(bf16[2,3,64,32]{2,3,1,0:T(8,128)(2,1)} %param.24) | copy-start | bytes 73732
  305.8 36.4 %collective-permute-start.2 = (bf16[1,30,1,64]{3,2,1,0:T(2,128)(2,1)S(1)}, bf16[1,30,1,64]{3,2,1,0:T(2,128)(2,1)S(1)}, u32[]{:S(2)}, u32[]{:S(2)}) collective-permute-start(bf16[1,30,1,64]{3,2,1,0:T(2,128)(2,1)S(1)} %get-tuple-element.71), channel_id=1, source_target_pairs={{0,1},{2,3},{4,5},{6,7},{8,9},{10,11},{12,13},{14,15},{16,17},{18,... | collective-permute-start | bytes 11528 | tf_op jit(solution)/shard_map/ppermute | solution.py:20
  307.1 35.1 %collective-permute-start.3 = (bf16[1,30,1,64]{3,2,1,0:T(2,128)(2,1)S(1)}, bf16[1,30,1,64]{3,2,1,0:T(2,128)(2,1)S(1)}, u32[]{:S(2)}, u32[]{:S(2)}) collective-permute-start(bf16[1,30,1,64]{3,2,1,0:T(2,128)(2,1)S(1)} %get-tuple-element.70), channel_id=1, source_target_pairs={{1,0},{3,2},{5,4},{7,6},{9,8},{11,10},{13,12},{15,14},{17,16},{19,... | collective-permute-start | bytes 11528 | tf_op jit(solution)/shard_map/ppermute | solution.py:22
  386.9 43.2 %copy-start.14 = (bf16[64,256]{0,1:T(8,128)(2,1)S(1)}, bf16[64,256]{0,1:T(8,128)(2,1)}, u32[]{:S(2)}) copy-start(bf16[64,256]{0,1:T(8,128)(2,1)} %all_gather.90) | copy-start | bytes 98308
  469.3 41.1 %copy-start.38 = (f32[1,256]{1,0:T(1,128)S(1)}, f32[1,256]{1,0:T(1,128)}, u32[]{:S(2)}) copy-start(f32[1,256]{1,0:T(1,128)} %get-tuple-element.108) | copy-start | bytes 3076
  592.0 4.3 copy-start.24
  592.1 38.0 %collective-permute-start.4 = (bf16[1,1,28,64]{3,2,1,0:T(8,128)(2,1)S(1)}, bf16[1,1,28,64]{3,2,1,0:T(8,128)(2,1)S(1)}, u32[]{:S(2)}, u32[]{:S(2)}) collective-permute-start(bf16[1,1,28,64]{3,2,1,0:T(8,128)(2,1)S(1)} %get-tuple-element.81), channel_id=1, source_target_pairs={{0,2},{1,3},{4,6},{5,7},{8,10},{9,11},{12,14},{13,15},{16,18},{17,... | collective-permute-start | bytes 10760 | tf_op jit(solution)/shard_map/ppermute | solution.py:20
  628.8 5.5 collective-permute-start.5
  634.5 34.3 %collective-permute-start.6 = (bf16[1,30,1,64]{3,2,1,0:T(2,128)(2,1)S(1)}, bf16[1,30,1,64]{3,2,1,0:T(2,128)(2,1)S(1)}, u32[]{:S(2)}, u32[]{:S(2)}) collective-permute-start(bf16[1,30,1,64]{3,2,1,0:T(2,128)(2,1)S(1)} %get-tuple-element.66), channel_id=1, source_target_pairs={{0,1},{2,3},{4,5},{6,7},{8,9},{10,11},{12,13},{14,15},{16,17},{18,... | collective-permute-start | bytes 11528 | tf_op jit(solution)/shard_map/ppermute | solution.py:20
  635.8 33.0 %collective-permute-start.7 = (bf16[1,30,1,64]{3,2,1,0:T(2,128)(2,1)S(1)}, bf16[1,30,1,64]{3,2,1,0:T(2,128)(2,1)S(1)}, u32[]{:S(2)}, u32[]{:S(2)}) collective-permute-start(bf16[1,30,1,64]{3,2,1,0:T(2,128)(2,1)S(1)} %get-tuple-element.65), channel_id=1, source_target_pairs={{1,0},{3,2},{5,4},{7,6},{9,8},{11,10},{13,12},{15,14},{17,16},{19,... | collective-permute-start | bytes 11528 | tf_op jit(solution)/shard_map/ppermute | solution.py:22
  715.2 42.1 %copy-start.13 = (bf16[64,256]{0,1:T(8,128)(2,1)S(1)}, bf16[64,256]{0,1:T(8,128)(2,1)}, u32[]{:S(2)}) copy-start(bf16[64,256]{0,1:T(8,128)(2,1)} %all_gather.99) | copy-start | bytes 98308
  797.3 40.9 %copy-start.36 = (f32[1,256]{1,0:T(1,128)S(1)}, f32[1,256]{1,0:T(1,128)}, u32[]{:S(2)}) copy-start(f32[1,256]{1,0:T(1,128)} %get-tuple-element.107) | copy-start | bytes 3076
  919.2 38.0 %collective-permute-start.8 = (bf16[1,1,28,64]{3,2,1,0:T(8,128)(2,1)S(1)}, bf16[1,1,28,64]{3,2,1,0:T(8,128)(2,1)S(1)}, u32[]{:S(2)}, u32[]{:S(2)}) collective-permute-start(bf16[1,1,28,64]{3,2,1,0:T(8,128)(2,1)S(1)} %get-tuple-element.76), channel_id=1, source_target_pairs={{0,2},{1,3},{4,6},{5,7},{8,10},{9,11},{12,14},{13,15},{16,18},{17,... | collective-permute-start | bytes 10760 | tf_op jit(solution)/shard_map/ppermute | solution.py:20
  955.9 5.5 collective-permute-start.9
  961.6 2.6 copy-start.23
  961.6 37.7 %collective-permute-start.10 = (bf16[1,30,1,64]{3,2,1,0:T(2,128)(2,1)S(1)}, bf16[1,30,1,64]{3,2,1,0:T(2,128)(2,1)S(1)}, u32[]{:S(2)}, u32[]{:S(2)}) collective-permute-start(bf16[1,30,1,64]{3,2,1,0:T(2,128)(2,1)S(1)} %get-tuple-element.61), channel_id=1, source_target_pairs={{0,1},{2,3},{4,5},{6,7},{8,9},{10,11},{12,13},{14,15},{16,17},{18,... | collective-permute-start | bytes 11528 | tf_op jit(solution)/shard_map/ppermute | solution.py:20
  962.9 36.4 %collective-permute-start.11 = (bf16[1,30,1,64]{3,2,1,0:T(2,128)(2,1)S(1)}, bf16[1,30,1,64]{3,2,1,0:T(2,128)(2,1)S(1)}, u32[]{:S(2)}, u32[]{:S(2)}) collective-permute-start(bf16[1,30,1,64]{3,2,1,0:T(2,128)(2,1)S(1)} %get-tuple-element.60), channel_id=1, source_target_pairs={{1,0},{3,2},{5,4},{7,6},{9,8},{11,10},{13,12},{15,14},{17,16},{19,... | collective-permute-start | bytes 11528 | tf_op jit(solution)/shard_map/ppermute | solution.py:22
  1043.5 42.1 %copy-start.15 = (bf16[64,256]{0,1:T(8,128)(2,1)S(1)}, bf16[64,256]{0,1:T(8,128)(2,1)}, u32[]{:S(2)}) copy-start(bf16[64,256]{0,1:T(8,128)(2,1)} %all_gather.108) | copy-start | bytes 98308
  1125.7 40.9 %copy-start.40 = (f32[1,256]{1,0:T(1,128)S(1)}, f32[1,256]{1,0:T(1,128)}, u32[]{:S(2)}) copy-start(f32[1,256]{1,0:T(1,128)} %get-tuple-element.109) | copy-start | bytes 3076
  (46 other events, 32.9 us)
